TPU v7x, 32 devices: a whole 2x2x4 slice. The times are simulated.
32 devices in a mesh: row: 8 (over y, x, core), col: 4 (over z).
Axes of the slice: x: 2, y: 2, z: 4, core: 2. Of those that a mesh axis runs over, the one named last changes fastest.
Arguments:
- sources: float32 [8, 4, 512, 512], P('row', 'col'), may hold values from -6 to 6
- leaf_basis: float32 [8, 4, 512, 256], P('row', 'col'), may hold values from -0.25 to 0.25
- transfers: float32 [8, 4, 4, 256, 512], P('row', 'col'), may hold values from -0.25 to 0.25
- out_basis: float32 [8, 4, 512, 256], P('row', 'col'), may hold values from -0.375 to 0.375
Outputs:
- result: float32 [8, 4, 512, 512], P('row', 'col')
All inputs are finite; a program needn't handle non-finite values.
Results may differ from a plain program's by a relative error of at most 0.0001.
Values sent between devices are 32-bit elements; how exact they have to be, the bound alone decides.
A program may use at most 64 MiB of HBM per device.

v0:
```python
import jax
import jax.numpy as jnp
from jax import lax
from jax.experimental import pallas as pl
from jax.experimental.pallas import tpu as pltpu
from jax.sharding import PartitionSpec as P

GROUP = 128
CHUNK = 64
LAGS = (320, 160)
RAMP = (32, 32, 64)
WIDE = 512


def split(x):
    high = x.astype(jnp.bfloat16)
    return high, (x - high.astype(jnp.float32)).astype(jnp.bfloat16)


def product(left, right_high, right_low, right_dim):
    dims = (((1,), (right_dim,)), ((), ()))
    rows = left.shape[0]
    high, low = split(left)
    both = lax.dot_general(
        jnp.concatenate([high, low], axis=0), right_high, dims, preferred_element_type=jnp.float32
    )
    rest = lax.dot_general(high, right_low, dims, preferred_element_type=jnp.float32)
    return both[:rows] + (both[rows:] + rest)


def chunks_of(rhs):
    body = rhs - 2 * sum(RAMP)
    sizes = list(RAMP) + [CHUNK] * (body // CHUNK)
    if body % CHUNK:
        sizes.append(body % CHUNK)
    sizes += list(RAMP)[::-1]
    starts = [sum(sizes[:at]) for at in range(len(sizes))]
    return list(zip(starts, sizes))


def order_of(chunks, levels):
    steps = []
    for at, (start, size) in enumerate(chunks):
        for level in range(levels):
            lag = LAGS[0] * ((level + 1) // 2) + LAGS[1] * (level // 2)
            steps.append((start + lag, -level, at, level))
    return [(at, -low) for _, low, at, _ in sorted(steps)]


def partner(level, levels):
    axis = "row" if level % 2 == 0 else "col"
    span = lax.axis_size(axis) >> (1 + level // 2)
    me = lax.axis_index(axis)
    return {axis: me + span - 2 * span * ((me // span) % 2)}


def kernel(
    src, leaf, tra, res,
    src_v, leaf_v, tra_v, coeff, other, t_high, t_low,
    in_sem, tra_sem, out_sem, send_sem, recv_sem,
):
    levels, rank = tra.shape[0], leaf.shape[1]
    rhs = src.shape[1]
    groups = rhs // GROUP
    chunks = chunks_of(rhs)
    partners = [partner(level, levels) for level in range(levels)]

    barrier = pltpu.get_barrier_semaphore()
    for who in partners:
        pl.semaphore_signal(barrier, inc=1, device_id=who, device_id_type=pl.DeviceIdType.MESH)

    load_leaf = pltpu.make_async_copy(leaf, leaf_v, in_sem.at[groups])
    load_leaf.start()
    load_src = []
    for g in range(groups):
        cols = pl.ds(g * GROUP, GROUP)
        load_src.append(pltpu.make_async_copy(src.at[:, cols], src_v.at[:, cols], in_sem.at[g]))
        load_src[-1].start()
    load_tra = [pltpu.make_async_copy(tra.at[k], tra_v.at[k], tra_sem.at[k]) for k in range(levels)]
    for copy in load_tra:
        copy.start()

    copies = {}

    def send(at, level):
        rows = pl.ds(*chunks[at])
        copy = pltpu.make_async_remote_copy(
            src_ref=coeff.at[level, rows],
            dst_ref=other.at[level, rows],
            send_sem=send_sem.at[level, at],
            recv_sem=recv_sem.at[level, at],
            device_id=partners[level],
            device_id_type=pl.DeviceIdType.MESH,
        )
        copy.start()
        copies[at, level] = copy

    load_leaf.wait()
    l_high, l_low = split(leaf_v[...])
    for g in range(groups):
        load_src[g].wait()
        turned = src_v[:, g * GROUP:(g + 1) * GROUP].T
        coeff[0, pl.ds(g * GROUP, GROUP), :] = product(turned, l_high, l_low, 0)
        if g == 0:
            pl.semaphore_wait(barrier, levels)
        for at, (start, size) in enumerate(chunks):
            if g * GROUP < start + size <= (g + 1) * GROUP:
                send(at, 0)
    def prepare(k):
        load_tra[k].wait()
        high, low = split(tra_v[k].T)
        t_high[k] = high
        t_low[k] = low

    def mix(k, left, half):
        part = slice(half * rank, (half + 1) * rank)
        return product(left, t_high[k, part, :], t_low[k, part, :], 0)

    prepared = 0

    stores = []
    for at, level in order_of(chunks, levels):
        rows = pl.ds(*chunks[at])
        if level == prepared:
            prepare(level)
            prepared += 1
        own = mix(level, coeff[level, rows, :], 0)
        copies[at, level].wait_recv()
        fresh = own + mix(level, other[level, rows, :], 1)
        coeff[level + 1, rows, :] = fresh
        if level + 1 < levels:
            send(at, level + 1)
            continue
        stores.append(pltpu.make_async_copy(coeff.at[levels, rows], res.at[rows], out_sem.at[at]))
        stores[-1].start()
    for copy in copies.values():
        copy.wait_send()
    for copy in stores:
        copy.wait()


def expand(last, outb, res):
    last_high, last_low = split(last[...])
    res[...] = product(outb[...], last_high, last_low, 1)


def body(sources, leaf_basis, transfers, out_basis):
    src, leaf, tra, outb = sources[0, 0], leaf_basis[0, 0], transfers[0, 0], out_basis[0, 0]
    size, rhs = src.shape
    rank = leaf.shape[1]
    count = len(chunks_of(rhs))
    levels = tra.shape[0]
    f32 = jnp.float32
    any_space = pl.BlockSpec(memory_space=pl.ANY)
    hbm = pl.BlockSpec(memory_space=pltpu.HBM)
    last = pl.pallas_call(
        kernel,
        out_shape=jax.ShapeDtypeStruct((rhs, rank), f32),
        in_specs=[hbm] * 3,
        out_specs=any_space,
        scratch_shapes=[
            pltpu.VMEM((size, rhs), f32),
            pltpu.VMEM((size, rank), f32),
            pltpu.VMEM(tra.shape, f32),
            pltpu.VMEM((levels + 1, rhs, rank), f32),
            pltpu.VMEM((levels, rhs, rank), f32),
            pltpu.VMEM((levels, 2 * rank, rank), jnp.bfloat16),
            pltpu.VMEM((levels, 2 * rank, rank), jnp.bfloat16),
            pltpu.SemaphoreType.DMA((rhs // GROUP + 1,)),
            pltpu.SemaphoreType.DMA((levels,)),
            pltpu.SemaphoreType.DMA((count,)),
            pltpu.SemaphoreType.DMA((levels, count)),
            pltpu.SemaphoreType.DMA((levels, count)),
        ],
        compiler_params=pltpu.CompilerParams(collective_id=0, has_side_effects=True),
    )(src, leaf, tra)
    wide = min(WIDE, rhs)
    result = pl.pallas_call(
        expand,
        grid=(rhs // wide,),
        out_shape=jax.ShapeDtypeStruct((size, rhs), f32),
        in_specs=[
            pl.BlockSpec((wide, rank), lambda i: (i, 0)),
            pl.BlockSpec((size, rank), lambda i: (0, 0)),
        ],
        out_specs=pl.BlockSpec((size, wide), lambda i: (0, i)),
    )(last, outb)
    return result[None, None]


def solution(mesh):
    in_specs = (
        P("row", "col", None, None),
        P("row", "col", None, None),
        P("row", "col", None, None, None),
        P("row", "col", None, None),
    )
    out_specs = P("row", "col", None, None)
    return jax.shard_map(body, mesh=mesh, in_specs=in_specs, out_specs=out_specs, check_vma=False)
```

profile of v0, /device:TPU:0, one launch (start us, length us, event | category | flops | bytes accessed | tf_op | source)
XLA Modules:
  0.0 43.7 jit_solution(10561884604751928815)
XLA Ops:
  0.0 40.9 %shard_map.46.last = f32[512,256]{1,0:T(8,128)} custom-call(f32[512,512]{1,0:T(8,128)} %bitcast.6, f32[512,256]{1,0:T(8,128)} %bitcast.8, f32[4,256,512]{2,1,0:T(8,128)} %bitcast.5), custom_call_target="tpu_custom_call" | custom-call | tf_op jit(solution)/shard_map/pallas_call | solution.py:156
  41.0 2.8 %shard_map.47 = f32[512,512]{1,0:T(8,128)} custom-call(f32[512,256]{1,0:T(8,128)} %shard_map.46.last, f32[512,256]{1,0:T(8,128)} %bitcast.7), custom_call_target="tpu_custom_call" | custom-call | tf_op jit(solution)/shard_map/pallas_call | solution.py:178
where the time goes:
time: 43.9 us; the launch traced here: 43.7 us
  Pallas kernels  43.7 us (100%)
    pallas_call x1, Pallas kernels, body(): pl.pallas_call(kernel, out_shape=jax.ShapeDtypeStruct((rhs, rank), f32),...  40.9 us
    pallas_call x1, Pallas kernels, body(): pl.pallas_call(expand, grid=(rhs // wide,), out_shape=jax.ShapeDtypeStruc...  2.78 us

commit v1 on v0

--- a/solution.py
+++ b/solution.py
@@ -7,9 +7,9 @@
 
 GROUP = 128
 CHUNK = 64
-LAGS = (320, 160)
+LAGS = (0, 256, 384, 576)
 RAMP = (32, 32, 64)
-WIDE = 512
+LIMIT = 8 * 2**20
 
 
 def split(x):
@@ -42,8 +42,7 @@
     steps = []
     for at, (start, size) in enumerate(chunks):
         for level in range(levels):
-            lag = LAGS[0] * ((level + 1) // 2) + LAGS[1] * (level // 2)
-            steps.append((start + lag, -level, at, level))
+            steps.append((start + LAGS[level], -level, at, level))
     return [(at, -low) for _, low, at, _ in sorted(steps)]
 
 
@@ -55,9 +54,9 @@
 
 
 def kernel(
-    src, leaf, tra, res,
-    src_v, leaf_v, tra_v, coeff, other, t_high, t_low,
-    in_sem, tra_sem, out_sem, send_sem, recv_sem,
+    src, leaf, tra, outb, res,
+    src_v, leaf_v, tra_v, outb_v, coeff, other, t_high, t_low, o_both,
+    in_sem, tra_sem, send_sem, recv_sem,
 ):
     levels, rank = tra.shape[0], leaf.shape[1]
     rhs = src.shape[1]
@@ -79,6 +78,8 @@
     load_tra = [pltpu.make_async_copy(tra.at[k], tra_v.at[k], tra_sem.at[k]) for k in range(levels)]
     for copy in load_tra:
         copy.start()
+    load_outb = pltpu.make_async_copy(outb, outb_v, in_sem.at[groups + 1])
+    load_outb.start()
 
     copies = {}
 
@@ -116,32 +117,54 @@
         part = slice(half * rank, (half + 1) * rank)
         return product(left, t_high[k, part, :], t_low[k, part, :], 0)
 
+    def expand(g):
+        high, low = split(coeff[levels, pl.ds(g * GROUP, GROUP), :])
+        dims = (((1,), (1,)), ((), ()))
+        wide = lax.dot_general(o_both[...], high, dims, preferred_element_type=jnp.float32)
+        rest = lax.dot_general(o_both[:size, :], low, dims, preferred_element_type=jnp.float32)
+        res[:, g * GROUP:(g + 1) * GROUP] = wide[:size] + (wide[size:] + rest)
+
     prepared = 0
-
-    stores = []
+    size = outb.shape[0]
+    ready = 0
+    missing = [sum(1 for start, n in chunks if start // GROUP == g) for g in range(groups)]
     for at, level in order_of(chunks, levels):
         rows = pl.ds(*chunks[at])
         if level == prepared:
             prepare(level)
             prepared += 1
         own = mix(level, coeff[level, rows, :], 0)
-        copies[at, level].wait_recv()
+        with jax.named_scope(f"w{level}_{at}"):
+            copies[at, level].wait_recv()
         fresh = own + mix(level, other[level, rows, :], 1)
         coeff[level + 1, rows, :] = fresh
         if level + 1 < levels:
             send(at, level + 1)
             continue
-        stores.append(pltpu.make_async_copy(coeff.at[levels, rows], res.at[rows], out_sem.at[at]))
-        stores[-1].start()
+        g = chunks[at][0] // GROUP
+        missing[g] -= 1
+        if ready == 0:
+            load_outb.wait()
+            high, low = split(outb_v[...])
+            o_both[:size, :] = high
+            o_both[size:, :] = low
+            ready = 1
+        if missing[g] == 0:
+            expand(g)
     for copy in copies.values():
         copy.wait_send()
-    for copy in stores:
-        copy.wait()
-
-
-def expand(last, outb, res):
-    last_high, last_low = split(last[...])
-    res[...] = product(outb[...], last_high, last_low, 1)
+
+
+def store(held, res, sem):
+    groups = sem.shape[0]
+    wide = held.shape[0] // groups
+    moves = []
+    for g in range(groups):
+        rows = pl.ds(g * wide, wide)
+        moves.append(pltpu.make_async_copy(held.at[rows], res.at[rows], sem.at[g]))
+        moves[-1].start()
+    for move in moves:
+        move.wait()
 
 
 def body(sources, leaf_basis, transfers, out_basis):
@@ -153,38 +176,38 @@
     f32 = jnp.float32
     any_space = pl.BlockSpec(memory_space=pl.ANY)
     hbm = pl.BlockSpec(memory_space=pltpu.HBM)
-    last = pl.pallas_call(
+    held = pl.pallas_call(
         kernel,
-        out_shape=jax.ShapeDtypeStruct((rhs, rank), f32),
-        in_specs=[hbm] * 3,
-        out_specs=any_space,
+        out_shape=pltpu.VMEM((size, rhs), f32),
+        in_specs=[hbm] * 4,
+        out_specs=pl.BlockSpec(memory_space=pltpu.VMEM),
         scratch_shapes=[
             pltpu.VMEM((size, rhs), f32),
             pltpu.VMEM((size, rank), f32),
             pltpu.VMEM(tra.shape, f32),
+            pltpu.VMEM((size, rank), f32),
             pltpu.VMEM((levels + 1, rhs, rank), f32),
             pltpu.VMEM((levels, rhs, rank), f32),
             pltpu.VMEM((levels, 2 * rank, rank), jnp.bfloat16),
             pltpu.VMEM((levels, 2 * rank, rank), jnp.bfloat16),
-            pltpu.SemaphoreType.DMA((rhs // GROUP + 1,)),
+            pltpu.VMEM((2 * size, rank), jnp.bfloat16),
+            pltpu.SemaphoreType.DMA((rhs // GROUP + 2,)),
             pltpu.SemaphoreType.DMA((levels,)),
-            pltpu.SemaphoreType.DMA((count,)),
             pltpu.SemaphoreType.DMA((levels, count)),
             pltpu.SemaphoreType.DMA((levels, count)),
         ],
-        compiler_params=pltpu.CompilerParams(collective_id=0, has_side_effects=True),
-    )(src, leaf, tra)
-    wide = min(WIDE, rhs)
+        compiler_params=pltpu.CompilerParams(
+            collective_id=0, has_side_effects=True
+        ),
+    )(src, leaf, tra, outb)
     result = pl.pallas_call(
-        expand,
-        grid=(rhs // wide,),
+        store,
         out_shape=jax.ShapeDtypeStruct((size, rhs), f32),
-        in_specs=[
-            pl.BlockSpec((wide, rank), lambda i: (i, 0)),
-            pl.BlockSpec((size, rank), lambda i: (0, 0)),
-        ],
-        out_specs=pl.BlockSpec((size, wide), lambda i: (0, i)),
-    )(last, outb)
+        in_specs=[pl.BlockSpec(memory_space=pltpu.VMEM)],
+        out_specs=any_space,
+        scratch_shapes=[pltpu.SemaphoreType.DMA((4,))],
+        compiler_params=pltpu.CompilerParams(vmem_limit_bytes=LIMIT),
+    )(held)
     return result[None, None]
 
 

time: 43.9 us -> 40.7 us (0.927)
  Pallas kernels: 43.7 us -> 40.5 us
    pallas_call x2, Pallas kernels: 43.7 us -> 40.5 us  [the longest x1 39.5 us: body(): pl.pallas_call(kernel, out_shape=pltpu.VMEM((size, rhs), f32), in_specs=[...]
where the time goes in v1:
time: 40.7 us; the launch traced here: 40.5 us
  Pallas kernels  40.5 us (100%)
    pallas_call x1, Pallas kernels, body(): pl.pallas_call(kernel, out_shape=pltpu.VMEM((size, rhs), f32), in_specs=[...  39.5 us
    pallas_call x1, Pallas kernels, body(): pl.pallas_call(store, out_shape=jax.ShapeDtypeStruct((size, rhs), f32), i...  1 us

profile of v1, /device:TPU:0, one launch (start us, length us, event | category | flops | bytes accessed | tf_op | source)
XLA Modules:
  0.0 40.5 jit_solution(12273356147953273836)
XLA Ops:
  0.0 39.5 %shard_map.46.held = f32[512,512]{1,0:T(8,128)S(1)} custom-call(f32[512,512]{1,0:T(8,128)} %bitcast.6, f32[512,256]{1,0:T(8,128)} %bitcast.7, f32[4,256,512]{2,1,0:T(8,128)} %bitcast.5, f32[512,256]{1,0:T(8,128)} %bitcast.8), custom_call_target="tpu_custom_call" | custom-call | tf_op jit(solution)/shard_map/pallas_call | solution.py:179
  39.5 1.0 %shard_map.47 = f32[512,512]{1,0:T(8,128)} custom-call(f32[512,512]{1,0:T(8,128)S(1)} %shard_map.46.held), custom_call_target="tpu_custom_call" | custom-call | tf_op jit(solution)/shard_map/pallas_call | solution.py:203

commit v2 on v0

v2 whole, which is shorter than its diff:
```python
import jax
import jax.numpy as jnp
from jax import lax
from jax.experimental import pallas as pl
from jax.experimental.pallas import tpu as pltpu
from jax.sharding import PartitionSpec as P

GROUP = 128
CHUNK = 64
FIRST = 128
LAGS = ((0, 240, 416, 672, 592), (0, 240, 256, 512, 496))
SLOPES = ((1, 1, 1, 1, 1.2), (1, 0.8, 1, 0.9, 1.0))
HEAD = (32, 32, 64)
TAIL = (64, 32, 32)
LIMIT = 8 * 2**20


def split(x):
    high = x.astype(jnp.bfloat16)
    return high, (x - high.astype(jnp.float32)).astype(jnp.bfloat16)


def product(left, right_high, right_low, right_dim):
    dims = (((1,), (right_dim,)), ((), ()))
    rows = left.shape[0]
    high, low = split(left)
    both = lax.dot_general(
        jnp.concatenate([high, low], axis=0), right_high, dims, preferred_element_type=jnp.float32
    )
    rest = lax.dot_general(high, right_low, dims, preferred_element_type=jnp.float32)
    return both[:rows] + (both[rows:] + rest)


def chunks_of(rhs):
    body = rhs - sum(HEAD) - sum(TAIL)
    sizes = list(HEAD) + [CHUNK] * (body // CHUNK)
    if body % CHUNK:
        sizes.append(body % CHUNK)
    sizes += list(TAIL)
    starts = [sum(sizes[:at]) for at in range(len(sizes))]
    return list(zip(starts, sizes))


def order_of(chunks, levels, lags, slopes):
    steps = []
    groups = chunks[-1][0] // GROUP + 1
    for at, (start, size) in enumerate(chunks):
        last = (start + size) % GROUP == 0 and start // GROUP + 1 < groups
        for level in range(levels + last):
            key = start * slopes[level] + lags[level]
            if level:
                key = max(key, steps[-1][0] + 1)
            steps.append((key, -level, at, level))
    return [(at, level) for _, _, at, level in sorted(steps)]


def expand(o_both, coeff):
    size = o_both.shape[0] // 2
    high, low = split(coeff)
    dims = (((1,), (1,)), ((), ()))
    wide = lax.dot_general(o_both[...], high, dims, preferred_element_type=jnp.float32)
    rest = lax.dot_general(o_both[:size, :], low, dims, preferred_element_type=jnp.float32)
    return wide[:size] + (wide[size:] + rest)


def partner(level, levels):
    axis = "row" if level % 2 == 0 else "col"
    span = lax.axis_size(axis) >> (1 + level // 2)
    me = lax.axis_index(axis)
    return {axis: me + span - 2 * span * ((me // span) % 2)}


def kernel(
    src, leaf, tra, outb, held, tail, o_both,
    src_v, leaf_v, tra_v, outb_v, coeff, other, t_high, t_low,
    in_sem, send_sem, recv_sem,
):
    levels, rank = tra.shape[0], leaf.shape[1]
    rhs = src.shape[1]
    groups = rhs // GROUP
    chunks = chunks_of(rhs)
    partners = [partner(level, levels) for level in range(levels)]

    barrier = pltpu.get_barrier_semaphore()
    for who in partners:
        pl.semaphore_signal(barrier, inc=1, device_id=who, device_id_type=pl.DeviceIdType.MESH)

    load_leaf = pltpu.make_async_copy(leaf, leaf_v, in_sem.at[0])
    load_leaf.start()
    load_src = []
    for at, cols in enumerate((pl.ds(0, GROUP), pl.ds(GROUP, rhs - GROUP))):
        load_src.append(pltpu.make_async_copy(src.at[:, cols], src_v.at[:, cols], in_sem.at[1 + at]))
        load_src[-1].start()
    load_tra = [
        pltpu.make_async_copy(tra.at[ks], tra_v.at[ks], in_sem.at[3 + at])
        for at, ks in enumerate((pl.ds(0, 1), pl.ds(1, levels - 1)))
    ]
    load_outb = pltpu.make_async_copy(outb, outb_v, in_sem.at[5])

    def copy_of(at, level):
        rows = pl.ds(*chunks[at])
        return pltpu.make_async_remote_copy(
            src_ref=coeff.at[level, rows],
            dst_ref=other.at[level, rows],
            send_sem=send_sem.at[0],
            recv_sem=recv_sem.at[level, at],
            device_id=partners[level],
            device_id_type=pl.DeviceIdType.MESH,
        )

    load_leaf.wait()
    l_high, l_low = split(leaf_v[...])
    for g in range(groups):
        if g < 2:
            load_src[g].wait()
        if g == 0:
            for copy in load_tra:
                copy.start()
            load_outb.start()
        turned = src_v[:, g * GROUP:(g + 1) * GROUP].T
        edges = (0, FIRST, GROUP) if g == 0 and FIRST < GROUP else (0, GROUP)
        for low, high in zip(edges[:-1], edges[1:]):
            rows = pl.ds(g * GROUP + low, high - low)
            coeff[0, rows, :] = product(turned[low:high], l_high, l_low, 0)
            if g + low == 0:
                pl.semaphore_wait(barrier, levels)
            for at, (start, size) in enumerate(chunks):
                if g * GROUP + low < start + size <= g * GROUP + high:
                    copy_of(at, 0).start()

    def prepare(k):
        if k < 2:
            load_tra[k].wait()
        if k == levels:
            load_outb.wait()
            high, low = split(outb_v[...])
            o_both[:size, :] = high
            o_both[size:, :] = low
            return
        high, low = split(tra_v[k].T)
        t_high[k] = high
        t_low[k] = low

    def mix(k, left, half):
        part = slice(half * rank, (half + 1) * rank)
        return product(left, t_high[k, part, :], t_low[k, part, :], 0)

    size = outb.shape[0]

    body_cols = rhs - tail.shape[0]

    def run(order):
        prepared = 0
        for step, (at, level) in enumerate(order):
            start, count = chunks[at]
            rows = pl.ds(start, count)
            if level == levels:
                cols = pl.ds(start // GROUP * GROUP, GROUP)
                with jax.named_scope(f"x{at}"):
                    held[:, cols] = expand(o_both, coeff[levels, cols, :])
                continue
            while prepared <= levels and (step >= prepared or level >= prepared):
                prepare(prepared)
                prepared += 1
            own = mix(level, coeff[level, rows, :], 0)
            with jax.named_scope(f"w{level}_{at}"):
                copy_of(at, level).wait_recv()
            fresh = own + mix(level, other[level, rows, :], 1)
            if level + 1 < levels:
                coeff[level + 1, rows, :] = fresh
                copy_of(at, level + 1).start()
            elif start < body_cols:
                coeff[levels, rows, :] = fresh
            else:
                tail[pl.ds(start - body_cols, count), :] = fresh

    core = lax.axis_index("row") % 2
    orders = [order_of(chunks, levels, *pair) for pair in zip(LAGS, SLOPES)]
    if orders[0] == orders[1]:
        run(orders[0])
    else:
        for k in range(2):
            pl.when(core == k)(lambda k=k: run(orders[k]))
    with jax.named_scope("end"):
        pltpu.make_async_remote_copy(
            src_ref=coeff.at[pl.ds(0, levels)],
            dst_ref=other,
            send_sem=send_sem.at[0],
            recv_sem=recv_sem.at[0, 0],
            device_id=partners[0],
            device_id_type=pl.DeviceIdType.MESH,
        ).wait_send()


def store(held, tail, o_both, res, last, sem):
    done = held.shape[1]
    early = pltpu.make_async_copy(held, res.at[:, pl.ds(0, done)], sem.at[0])
    early.start()
    last[...] = expand(o_both, tail[...])
    late = pltpu.make_async_copy(last, res.at[:, pl.ds(done, last.shape[1])], sem.at[1])
    late.start()
    early.wait()
    late.wait()


def body(sources, leaf_basis, transfers, out_basis):
    src, leaf, tra, outb = sources[0, 0], leaf_basis[0, 0], transfers[0, 0], out_basis[0, 0]
    size, rhs = src.shape
    rank = leaf.shape[1]
    count = len(chunks_of(rhs))
    levels = tra.shape[0]
    f32 = jnp.float32
    any_space = pl.BlockSpec(memory_space=pl.ANY)
    hbm = pl.BlockSpec(memory_space=pltpu.HBM)
    vmem = pl.BlockSpec(memory_space=pltpu.VMEM)
    parts = pl.pallas_call(
        kernel,
        out_shape=[
            pltpu.VMEM((size, rhs - GROUP), f32),
            pltpu.VMEM((GROUP, rank), f32),
            pltpu.VMEM((2 * size, rank), jnp.bfloat16),
        ],
        in_specs=[hbm] * 4,
        out_specs=[vmem] * 3,
        scratch_shapes=[
            pltpu.VMEM((size, rhs), f32),
            pltpu.VMEM((size, rank), f32),
            pltpu.VMEM(tra.shape, f32),
            pltpu.VMEM((size, rank), f32),
            pltpu.VMEM((levels + 1, rhs, rank), f32),
            pltpu.VMEM((levels, rhs, rank), f32),
            pltpu.VMEM((levels, 2 * rank, rank), jnp.bfloat16),
            pltpu.VMEM((levels, 2 * rank, rank), jnp.bfloat16),
            pltpu.SemaphoreType.DMA((6,)),
            pltpu.SemaphoreType.DMA((1,)),
            pltpu.SemaphoreType.DMA((levels, count)),
        ],
        compiler_params=pltpu.CompilerParams(
            collective_id=0, has_side_effects=True
        ),
    )(src, leaf, tra, outb)
    result = pl.pallas_call(
        store,
        out_shape=jax.ShapeDtypeStruct((size, rhs), f32),
        in_specs=[vmem] * 3,
        out_specs=any_space,
        scratch_shapes=[pltpu.VMEM((size, GROUP), f32), pltpu.SemaphoreType.DMA((2,))],
        compiler_params=pltpu.CompilerParams(vmem_limit_bytes=LIMIT),
    )(*parts)
    return result[None, None]


def solution(mesh):
    in_specs = (
        P("row", "col", None, None),
        P("row", "col", None, None),
        P("row", "col", None, None, None),
        P("row", "col", None, None),
    )
    out_specs = P("row", "col", None, None)
    return jax.shard_map(body, mesh=mesh, in_specs=in_specs, out_specs=out_specs, check_vma=False)
```

time: 43.9 us -> 39.2 us (0.89); the launches traced: 43.7 us -> 38.6 us
  Pallas kernels: 43.7 us -> 38.4 us
    pallas_call x2, Pallas kernels: 43.7 us -> 38.4 us  [the longest x1 37.3 us: body(): pl.pallas_call(kernel, out_shape=[pltpu.VMEM((size, rhs - GROUP), f32), p...]
where the time goes in v2:
time: 39.2 us; the launch traced here: 38.6 us
  Pallas kernels  38.4 us (98%)
    pallas_call x1, Pallas kernels, body(): pl.pallas_call(kernel, out_shape=[pltpu.VMEM((size, rhs - GROUP), f32), p...  37.3 us
    pallas_call x1, Pallas kernels, body(): pl.pallas_call(store, out_shape=jax.ShapeDtypeStruct((size, rhs), f32), i...  1.09 us

profile of v2, /device:TPU:0, one launch (start us, length us, event | category | flops | bytes accessed | tf_op | source)
XLA Modules:
  0.0 38.6 jit_solution(10432573370179630387)
XLA Ops:
  0.0 37.3 %shard_map.46 = (f32[512,384]{1,0:T(8,128)S(1)}, f32[128,256]{1,0:T(8,128)S(1)}, bf16[1024,256]{1,0:T(8,128)(2,1)S(1)}) custom-call(f32[512,512]{1,0:T(8,128)} %bitcast.6, f32[512,256]{1,0:T(8,128)} %bitcast.7, f32[4,256,512]{2,1,0:T(8,128)} %bitcast.5, f32[512,256]{1,0:T(8,128)} %bitcast.8), custom_call_target="tpu_custom_call" | custom-call | tf_op jit(solution)/shard_map/pallas_call | solution.py:216
  37.3 1.1 %shard_map.47 = f32[512,512]{1,0:T(8,128)} custom-call(f32[512,384]{1,0:T(8,128)S(1)} %get-tuple-element.8.held, f32[128,256]{1,0:T(8,128)S(1)} %get-tuple-element.9.tail, bf16[1024,256]{1,0:T(8,128)(2,1)S(1)} %get-tuple-element.10.o_both), custom_call_target="tpu_custom_call" | custom-call | tf_op jit(solution)/shard_map/pallas_call | solution.py:242

commit v3 on v2

--- a/solution.py
+++ b/solution.py
@@ -7,11 +7,12 @@
 
 GROUP = 128
 CHUNK = 64
-FIRST = 128
-LAGS = ((0, 240, 416, 672, 592), (0, 240, 256, 512, 496))
+FIRST = 64
+EARLY = 1
+LAGS = ((0, 240, 416, 672, 720), (0, 240, 256, 512, 496))
 SLOPES = ((1, 1, 1, 1, 1.2), (1, 0.8, 1, 0.9, 1.0))
 HEAD = (32, 32, 64)
-TAIL = (64, 32, 32)
+TAIL = (64, 40, 24)
 LIMIT = 8 * 2**20
 
 
@@ -54,13 +55,11 @@
     return [(at, level) for _, _, at, level in sorted(steps)]
 
 
-def expand(o_both, coeff):
-    size = o_both.shape[0] // 2
+def expand(o_cat, coeff):
     high, low = split(coeff)
+    both = jnp.concatenate([high, low, high], axis=1)
     dims = (((1,), (1,)), ((), ()))
-    wide = lax.dot_general(o_both[...], high, dims, preferred_element_type=jnp.float32)
-    rest = lax.dot_general(o_both[:size, :], low, dims, preferred_element_type=jnp.float32)
-    return wide[:size] + (wide[size:] + rest)
+    return lax.dot_general(o_cat[...], both, dims, preferred_element_type=jnp.float32)
 
 
 def partner(level, levels):
@@ -71,7 +70,7 @@
 
 
 def kernel(
-    src, leaf, tra, outb, held, tail, o_both,
+    src, leaf, tra, outb, held, tail, o_cat,
     src_v, leaf_v, tra_v, outb_v, coeff, other, t_high, t_low,
     in_sem, send_sem, recv_sem,
 ):
@@ -134,8 +133,9 @@
         if k == levels:
             load_outb.wait()
             high, low = split(outb_v[...])
-            o_both[:size, :] = high
-            o_both[size:, :] = low
+            o_cat[:, :rank] = high
+            o_cat[:, rank:2 * rank] = high
+            o_cat[:, 2 * rank:] = low
             return
         high, low = split(tra_v[k].T)
         t_high[k] = high
@@ -157,7 +157,7 @@
             if level == levels:
                 cols = pl.ds(start // GROUP * GROUP, GROUP)
                 with jax.named_scope(f"x{at}"):
-                    held[:, cols] = expand(o_both, coeff[levels, cols, :])
+                    held[:, cols] = expand(o_cat, coeff[levels, cols, :])
                 continue
             while prepared <= levels and (step >= prepared or level >= prepared):
                 prepare(prepared)
@@ -192,14 +192,19 @@
         ).wait_send()
 
 
-def store(held, tail, o_both, res, last, sem):
+def store(held, tail, o_cat, res, last, sem):
     done = held.shape[1]
-    early = pltpu.make_async_copy(held, res.at[:, pl.ds(0, done)], sem.at[0])
-    early.start()
-    last[...] = expand(o_both, tail[...])
-    late = pltpu.make_async_copy(last, res.at[:, pl.ds(done, last.shape[1])], sem.at[1])
+    part = held.shape[0] // EARLY
+    early = []
+    for at in range(EARLY):
+        rows = pl.ds(at * part, part)
+        early.append(pltpu.make_async_copy(held.at[rows], res.at[rows, pl.ds(0, done)], sem.at[1 + at]))
+        early[-1].start()
+    last[...] = expand(o_cat, tail[...])
+    late = pltpu.make_async_copy(last, res.at[:, pl.ds(done, last.shape[1])], sem.at[0])
     late.start()
-    early.wait()
+    for copy in early:
+        copy.wait()
     late.wait()
 
 
@@ -218,7 +223,7 @@
         out_shape=[
             pltpu.VMEM((size, rhs - GROUP), f32),
             pltpu.VMEM((GROUP, rank), f32),
-            pltpu.VMEM((2 * size, rank), jnp.bfloat16),
+            pltpu.VMEM((size, 3 * rank), jnp.bfloat16),
         ],
         in_specs=[hbm] * 4,
         out_specs=[vmem] * 3,
@@ -244,7 +249,7 @@
         out_shape=jax.ShapeDtypeStruct((size, rhs), f32),
         in_specs=[vmem] * 3,
         out_specs=any_space,
-        scratch_shapes=[pltpu.VMEM((size, GROUP), f32), pltpu.SemaphoreType.DMA((2,))],
+        scratch_shapes=[pltpu.VMEM((size, GROUP), f32), pltpu.SemaphoreType.DMA((1 + EARLY,))],
         compiler_params=pltpu.CompilerParams(vmem_limit_bytes=LIMIT),
     )(*parts)
     return result[None, None]

time: 39.2 us -> 39.2 us (level); the launches traced: 38.6 us -> 39 us
  Pallas kernels: 38.4 us -> 38.8 us
    pallas_call x1, Pallas kernels: 37.3 us -> 37.8 us  [body(): pl.pallas_call(kernel, out_shape=[pltpu.VMEM((size, rhs - GROUP), f32), p...]
where the time goes in v3:
time: 39.2 us; the launch traced here: 39 us
  Pallas kernels  38.8 us (99%)
    pallas_call x1, Pallas kernels, body(): pl.pallas_call(kernel, out_shape=[pltpu.VMEM((size, rhs - GROUP), f32), p...  37.8 us
    pallas_call x1, Pallas kernels, body(): pl.pallas_call(store, out_shape=jax.ShapeDtypeStruct((size, rhs), f32), i...  1.09 us

profile of v3, /device:TPU:0, one launch (start us, length us, event | category | flops | bytes accessed | tf_op | source)
XLA Modules:
  0.0 39.0 jit_solution(18106361958895395987)
XLA Ops:
  0.0 37.8 %shard_map.46 = (f32[512,384]{1,0:T(8,128)S(1)}, f32[128,256]{1,0:T(8,128)S(1)}, bf16[512,768]{1,0:T(8,128)(2,1)S(1)}) custom-call(f32[512,512]{1,0:T(8,128)} %bitcast.6, f32[512,256]{1,0:T(8,128)} %bitcast.7, f32[4,256,512]{2,1,0:T(8,128)} %bitcast.5, f32[512,256]{1,0:T(8,128)} %bitcast.8), custom_call_target="tpu_custom_call" | custom-call | tf_op jit(solution)/shard_map/pallas_call | solution.py:221
  37.8 1.1 %shard_map.47 = f32[512,512]{1,0:T(8,128)} custom-call(f32[512,384]{1,0:T(8,128)S(1)} %get-tuple-element.8.held, f32[128,256]{1,0:T(8,128)S(1)} %get-tuple-element.9.tail, bf16[512,768]{1,0:T(8,128)(2,1)S(1)} %get-tuple-element.10.o_cat), custom_call_target="tpu_custom_call" | custom-call | tf_op jit(solution)/shard_map/pallas_call | solution.py:247
